TPU v7x, 32 devices: a whole 2x2x4 slice. The times are simulated.
32 devices in a mesh: tensor: 4 (over y, core), context: 8 (over z, x).
Axes of the slice: x: 2, y: 2, z: 4, core: 2. Of those that a mesh axis runs over, the one named last changes fastest.
Arguments:
- query_rows: bfloat16 [2048, 8192], P('context', 'tensor'), may hold values from -160 to 160, as said below
- key_rows: bfloat16 [2048, 1024], P('context'), may hold values from -5 to 5, as said below
- value_rows: bfloat16 [2048, 1024], P('context'), may hold values from -6 to 6
- doc_ids: int32 [2048], P('context'), may hold values from 0 to 3, never falling along the last dimension, each value on 1 to 1024 neighbouring positions
- out_weight: bfloat16 [8192, 8192], P('tensor'), may hold values from -0.09375 to 0.09375
Outputs:
- mixed: bfloat16 [2048, 8192], P('context', 'tensor')
Inputs may be any that keep to these rules, and one draw needn't show every extreme that they name: `query_rows`: within the range given by the table of arrays. `key_rows`: within the range given by the table of arrays. `doc_ids`: document numbers never fall along the sequence; every document has 1 to 1024 tokens and one has exactly 1024.
All inputs are finite; a program needn't handle non-finite values.
Results may differ from a plain program's by a relative error of at most 0.015.
Values may be sent and summed in bfloat16 or wider, within the bound.
A program may use at most 128 MiB of HBM per device.

v0:
```python
import functools
import math

import jax
import jax.numpy as jnp
from jax import lax
from jax.experimental import pallas as pl
from jax.experimental.pallas import tpu as pltpu
from jax.sharding import PartitionSpec as P

H = 64
KVH = 8
HD = 128
DOC_MOST = 1024
REACH = 4
NEG_BIG = -1e30
PLACE = {0: 4, 2: 3, 1: 2, 3: 1, 4: 0}
EARLY = 3
MESH = pl.DeviceIdType.MESH
CHUNK = 512


def kernel(
    n_tensor, n_context, kv_count, per_kv, steps, chunks,
    query_hbm, key_hbm, value_hbm, doc_ref, weight_hbm, out_ref,
    query, kv, docs, bias, early_top, early_sum, att, weight, own, pair_out, pair_in, chip_out, chip_in,
    load_sem, kv_load_sem, weight_sem, kv_send, kv_recv, doc_send, doc_recv,
    pair_send, pair_recv, chip_send, chip_recv,
):
    tensor = lax.axis_index("tensor")
    context = lax.axis_index("context")
    chip, core = tensor // 2, tensor % 2
    partner = chip * 2 + (1 - core)
    n_chip = n_tensor // 2
    tok = query.shape[0]
    cols = chunks * own.shape[-1]
    width = own.shape[-1]
    even = context % 2 == 0
    odd = context % 2 == 1
    first_kv = tensor * (kv_count * per_kv) // (H // KVH) if per_kv * kv_count < H // KVH else tensor * kv_count
    OWN = PLACE[0]

    kv_loads = []
    for g in range(kv_count):
        at = pl.ds(pl.multiple_of((first_kv + g) * HD, HD), HD)
        mine = kv.at[g, pl.ds(OWN * tok, tok)]
        pair = (
            pltpu.make_async_copy(key_hbm.at[:, at], mine.at[:, pl.ds(0, HD)], kv_load_sem.at[g, 0]),
            pltpu.make_async_copy(value_hbm.at[:, at], mine.at[:, pl.ds(HD, HD)], kv_load_sem.at[g, 1]),
        )
        for c in pair:
            c.start()
        kv_loads.append(pair)
    query_load = pltpu.make_async_copy(query_hbm, query, load_sem)
    query_load.start()

    barrier = pltpu.get_barrier_semaphore()
    heard = jnp.int32(n_chip)
    for d in range(1, REACH + 1):
        for away in (d, -d):
            there = context + away
            ok = (there >= 0) & (there < n_context)
            heard = heard + jnp.where(ok, 1, 0).astype(jnp.int32)

            @pl.when(ok)
            def _():
                pl.semaphore_signal(barrier, inc=1, device_id={"tensor": tensor, "context": there}, device_id_type=MESH)

    pl.semaphore_signal(barrier, inc=1, device_id={"tensor": partner, "context": context}, device_id_type=MESH)
    for d in range(1, n_chip):
        to = lax.rem(chip + d, n_chip) * 2 + core
        pl.semaphore_signal(barrier, inc=1, device_id={"tensor": to, "context": context}, device_id_type=MESH)
    pl.semaphore_wait(barrier, heard)

    def kv_copy(from_slot, to_slot, kind, g, there):
        return pltpu.make_async_remote_copy(
            src_ref=kv.at[g, pl.ds(from_slot * tok, tok)],
            dst_ref=kv.at[g, pl.ds(to_slot * tok, tok)],
            send_sem=kv_send.at[kind, g],
            recv_sem=kv_recv.at[to_slot, g],
            device_id={"tensor": tensor, "context": there},
            device_id_type=MESH,
        )

    def doc_copy(d):
        return pltpu.make_async_remote_copy(
            src_ref=doc_ref,
            dst_ref=docs.at[PLACE[d]],
            send_sem=doc_send.at[d - 1],
            recv_sem=doc_recv.at[PLACE[d]],
            device_id={"tensor": tensor, "context": context + d},
            device_id_type=MESH,
        )

    def hops(g):
        ahead = context + 2 < n_context
        return {
            0: [
                (ahead, lambda: kv_copy(OWN, PLACE[2], 0, g, context + 2)),
                (even, lambda: kv_copy(OWN, PLACE[1], 1, g, context + 1)),
            ],
            2: [
                (odd & (context >= 2), lambda: kv_copy(PLACE[2], PLACE[1], 3, g, context - 1)),
                (ahead & (context >= 2), lambda: kv_copy(PLACE[2], PLACE[4], 2, g, context + 2)),
                (even & (context >= 2), lambda: kv_copy(PLACE[2], PLACE[3], 4, g, context + 1)),
            ],
            4: [(odd & (context >= 4), lambda: kv_copy(PLACE[4], PLACE[3], 5, g, context - 1))],
        }

    def launch(g, distance):
        for ok, c in hops(g)[distance]:
            @pl.when(ok)
            def _():
                c().start()

    def arrive(g, distance):
        @pl.when(context >= distance)
        def _():
            kv_copy(OWN, PLACE[distance], 0, g, context).wait_recv()

    for d in range(1, REACH + 1):
        @pl.when(context + d < n_context)
        def _():
            doc_copy(d).start()

    for g in range(kv_count):
        for c in kv_loads[g]:
            c.wait()
        launch(g, 0)

    def weight_copy(i, half):
        to = lax.rem(chip + 1 + i // chunks, n_chip) * 2 + (core if half == 0 else 1 - core)
        at = to * cols + lax.rem(i, chunks) * width
        return pltpu.make_async_copy(
            weight_hbm.at[:, pl.ds(pl.multiple_of(at, 128), width)], weight.at[i, half], weight_sem.at[i, half]
        )

    @pl.loop(0, steps)
    def _(i):
        weight_copy(i, 1).start()
        weight_copy(i, 0).start()

    for d in range(1, REACH + 1):
        @pl.when(context < d)
        def _():
            docs[PLACE[d]] = jnp.full(docs.shape[1:], -1, jnp.int32)
            for g in range(kv_count):
                kv[g, pl.ds(PLACE[d] * tok, tok)] = jnp.zeros((tok, 2 * HD), kv.dtype)

    doc_row = doc_ref[...].astype(jnp.float32)
    doc_col = jnp.broadcast_to(doc_row, (tok, tok)).T
    causal = lax.broadcasted_iota(jnp.int32, (tok, tok), 1) <= lax.broadcasted_iota(jnp.int32, (tok, tok), 0)
    bias[:, pl.ds(OWN * tok, tok)] = jnp.where(causal & (doc_col == doc_row), 0.0, NEG_BIG)
    for d in range(1, REACH + 1):
        @pl.when(context >= d)
        def _():
            doc_copy(d).wait_recv()
        row = docs[PLACE[d]].astype(jnp.float32)
        bias[:, pl.ds(PLACE[d] * tok, tok)] = jnp.where(doc_col == row, 0.0, NEG_BIG)

    query_load.wait()
    scale = HD ** -0.5 * math.log2(math.e)

    def weigh(p, g, keys):
        values = kv[g, keys, HD:]
        both = jnp.concatenate([values, jnp.ones_like(values)], axis=1)
        return jnp.dot(p.astype(jnp.bfloat16), both, preferred_element_type=jnp.float32)

    def score(q, g, keys, masked):
        return lax.dot_general(
            q, kv[g, keys, :HD], (((1,), (1,)), ((), ())), preferred_element_type=jnp.float32
        ) + masked

    def columns(head):
        return pl.ds(pl.multiple_of(head * HD, HD), HD)

    early = pl.ds(EARLY * tok, (REACH + 1 - EARLY) * tok)
    late = pl.ds(0, EARLY * tok)

    def attend_early(g, h):
        head = g * per_kv + h
        scores = score(query[:, columns(head)], g, early, bias[:, early])
        top = jnp.max(scores, axis=-1, keepdims=True)
        early_top[head] = jnp.broadcast_to(top, (tok, HD))
        early_sum[head] = weigh(jnp.exp2((scores - top) * scale), g, early)

    half_tok = tok // 2

    def attend_late(g, h, r):
        rows = pl.ds(r * half_tok, half_tok)
        heads = (g * per_kv + 2 * h, g * per_kv + 2 * h + 1)
        q = jnp.concatenate([query[rows, columns(head)] for head in heads], axis=0)
        scores = score(q, g, late, jnp.concatenate([bias[rows, late]] * 2, axis=0))
        before = jnp.concatenate([early_top[head, rows, :] for head in heads], axis=0)
        top = jnp.maximum(jnp.max(scores, axis=-1, keepdims=True), before[:, :1])
        sums = weigh(jnp.exp2((scores - top) * scale), g, late)
        sums = sums + jnp.exp2((before[:, :1] - top) * scale) * jnp.concatenate(
            [early_sum[head, rows, :] for head in heads], axis=0
        )
        done = (sums[:, :HD] / sums[:, HD:]).astype(jnp.bfloat16)
        att[rows, columns(heads[0])] = done[:half_tok]
        att[rows, columns(heads[1])] = done[half_tok:]

    def relay(g, distance):
        arrive(g, distance)
        launch(g, distance)

    for g in range(kv_count):
        relay(g, 2)
    for g in range(kv_count):
        @pl.loop(0, per_kv, unroll=2)
        def _(h):
            attend_early(g, h)

        relay(g, 4)

    def pair_copy(i, r):
        rows = pl.ds(r * half_tok, half_tok)
        return pltpu.make_async_remote_copy(
            src_ref=pair_out.at[i, rows], dst_ref=pair_in.at[i, rows],
            send_sem=pair_send.at[i, r], recv_sem=pair_recv.at[i, r],
            device_id={"tensor": partner, "context": context}, device_id_type=MESH,
        )

    def chip_copy(i, r):
        to = lax.rem(chip + 1 + i // chunks, n_chip) * 2 + core
        rows = pl.ds(r * half_tok, half_tok)
        return pltpu.make_async_remote_copy(
            src_ref=chip_out.at[i, rows], dst_ref=chip_in.at[i, rows],
            send_sem=chip_send.at[i, r], recv_sem=chip_recv.at[i, r],
            device_id={"tensor": to, "context": context}, device_id_type=MESH,
        )

    away = steps - chunks

    def project(i, r):
        rows = pl.ds(r * half_tok, half_tok)
        if r == 0:
            weight_copy(i, 1).wait()
        pair_out[i, rows] = jnp.dot(att[rows, :], weight[i, 1], preferred_element_type=jnp.float32).astype(jnp.bfloat16)
        pair_copy(i, r).start()
        if r == 0:
            weight_copy(i, 0).wait()
        own[i, rows] = jnp.dot(att[rows, :], weight[i, 0], preferred_element_type=jnp.float32).astype(jnp.bfloat16)

    def pair_sum(i, r):
        rows = pl.ds(r * half_tok, half_tok)
        pair_copy(i, r).wait_recv()
        return own[i, rows].astype(jnp.float32) + pair_in[i, rows].astype(jnp.float32)

    def forward(i, r):
        chip_out[i, pl.ds(r * half_tok, half_tok)] = pair_sum(i, r).astype(jnp.bfloat16)
        chip_copy(i, r).start()

    for r in range(2):
        for g in range(kv_count):
            if r == 0:
                arrive(g, 1)
                arrive(g, 3)

            @pl.loop(0, per_kv // 2, unroll=min(2, per_kv // 2))
            def _(h):
                attend_late(g, h, r)

        project(0, r)

        @pl.loop(1, away)
        def _(i):
            project(i, r)
            forward(i - 1, r)

        forward(away - 1, r)

    for r in range(2):
        @pl.loop(away, steps)
        def _(i):
            project(i, r)

    for r in range(2):
        for j in range(chunks):
            both = pair_sum(away + j, r)
            for d in range(n_chip - 1):
                chip_copy(d * chunks + j, r).wait_recv()
                both = both + chip_in[d * chunks + j, pl.ds(r * half_tok, half_tok)].astype(jnp.float32)
            out_ref[pl.ds(r * half_tok, half_tok), pl.ds(j * width, width)] = both.astype(out_ref.dtype)

    for d in range(1, REACH + 1):
        @pl.when(context + d < n_context)
        def _():
            doc_copy(d).wait_send()
    for g in range(kv_count):
        for distance in (0, 2, 4):
            for ok, c in hops(g)[distance]:
                @pl.when(ok)
                def _():
                    c().wait_send()

    @pl.loop(0, steps)
    def _(i):
        pair_copy(i, 0).wait_send()
        pair_copy(i, 1).wait_send()

    @pl.loop(0, away)
    def _(i):
        chip_copy(i, 0).wait_send()
        chip_copy(i, 1).wait_send()


def body(n_tensor, n_context, query_rows, key_rows, value_rows, doc_ids, out_weight):
    tok, local = query_rows.shape
    local_heads = local // HD
    group_size = H // KVH
    kv_count = max(1, local_heads // group_size)
    per_kv = local_heads // kv_count
    model = out_weight.shape[1]
    cols = model // n_tensor
    width = min(CHUNK, cols)
    chunks = cols // width
    n_chip = n_tensor // 2
    steps = n_chip * chunks
    assert n_tensor % 2 == 0 and n_context % 2 == 0 and cols % width == 0 and n_tensor > 2 and per_kv % 2 == 0
    assert REACH * tok >= DOC_MOST - 1
    bf = jnp.bfloat16
    dma = pltpu.SemaphoreType.DMA
    anywhere = pl.BlockSpec(memory_space=pl.ANY)
    inside = pl.BlockSpec(memory_space=pltpu.VMEM)
    away = steps - chunks
    return pl.pallas_call(
        functools.partial(kernel, n_tensor, n_context, kv_count, per_kv, steps, chunks),
        out_shape=jax.ShapeDtypeStruct((tok, cols), bf),
        in_specs=[anywhere, anywhere, anywhere, inside, anywhere],
        out_specs=inside,
        scratch_shapes=[
            pltpu.VMEM((tok, local), bf),
            pltpu.VMEM((kv_count, (REACH + 1) * tok, 2 * HD), bf),
            pltpu.VMEM((REACH, 1, tok), jnp.int32),
            pltpu.VMEM((tok, (REACH + 1) * tok), jnp.float32),
            pltpu.VMEM((local_heads, tok, HD), jnp.float32),
            pltpu.VMEM((local_heads, tok, 2 * HD), jnp.float32),
            pltpu.VMEM((tok, local), bf),
            pltpu.VMEM((steps, 2, local, width), bf),
            pltpu.VMEM((steps, tok, width), bf),
            pltpu.VMEM((steps, tok, width), bf),
            pltpu.VMEM((steps, tok, width), bf),
            pltpu.VMEM((max(away, 1), tok, width), bf),
            pltpu.VMEM((max(away, 1), tok, width), bf),
            dma,
            dma((kv_count, 2)),
            dma((steps, 2)),
            dma((6, kv_count)),
            dma((REACH, kv_count)),
            dma((REACH,)),
            dma((REACH,)),
            dma((steps, 2)),
            dma((steps, 2)),
            dma((max(away, 1), 2)),
            dma((max(away, 1), 2)),
        ],
        compiler_params=pltpu.CompilerParams(
            collective_id=0, has_side_effects=True, vmem_limit_bytes=62 * 1024 * 1024
        ),
    )(query_rows, key_rows, value_rows, doc_ids.reshape(1, tok), out_weight)


def solution(mesh):
    placed = (
        P("context", "tensor"),
        P("context", None),
        P("context", None),
        P("context"),
        P("tensor", None),
    )
    return jax.shard_map(
        functools.partial(body, mesh.shape["tensor"], mesh.shape["context"]),
        mesh=mesh, in_specs=placed, out_specs=P("context", "tensor"), check_vma=False,
    )
```

profile of v0, /device:TPU:16, one launch (start us, length us, event | category | flops | bytes accessed | tf_op | source)
XLA Modules:
  0.0 54.9 jit_solution(11533423175916106242)
XLA Ops:
  0.0 52.6 %shard_map.55 = bf16[256,2048]{1,0:T(8,128)(2,1)} custom-call(bf16[256,2048]{1,0:T(8,128)(2,1)} %query_hbm.1, bf16[256,1024]{1,0:T(8,128)(2,1)} %key_hbm.1, bf16[256,1024]{1,0:T(8,128)(2,1)} %value_hbm.1, s32[1,256]{1,0:T(1,128)} %bitcast.1, bf16[2048,8192]{1,0:T(8,128)(2,1)} %weight_hbm.1), custom_call_target="tpu_custom_call" | custom-call | tf_op jit(solution)/shard_map/pallas_call | solution.py:328
  52.6 2.3 %copy.7 = bf16[256,2048]{1,0:T(8,128)(2,1)} copy(bf16[256,2048]{1,0:T(8,128)(2,1)} %shard_map.55) | data formatting | bytes 2097152
where the time goes:
time: 55.1 us; the launch traced here: 54.9 us
  Pallas kernels  52.6 us (95%)
  local copies, waits for them, and re-layouts  2.3 us (4%)
    pallas_call x1, Pallas kernels, body(): pl.pallas_call(functools.partial(kernel, n_tensor, n_context, kv_count, p...  52.6 us
    unnamed x1, local copies, waits for them, and re-layouts  2.3 us

commit v1 on v0

v1 whole, which is shorter than its diff:
```python
import functools
import math

import jax
import jax.numpy as jnp
from jax import lax
from jax.experimental import pallas as pl
from jax.experimental.pallas import tpu as pltpu
from jax.sharding import PartitionSpec as P

H = 64
KVH = 8
HD = 128
DOC_MOST = 1024
REACH = 4
NEG_BIG = -1e30
MESH = pl.DeviceIdType.MESH
CHUNK = 512


def kernel(
    n_tensor, n_context, kv_count, per_kv, steps, chunks,
    query_hbm, key_hbm, value_hbm, doc_ref, weight_hbm, out_ref,
    query, kv, docs, bias, run_top, run_sum, att, weight, own, pair_out, pair_in, chip_out, chip_in,
    load_sem, kv_load_sem, weight_sem, kv_send, kv_recv, doc_send, doc_recv,
    pair_send, pair_recv, chip_send, chip_recv,
):
    tensor = lax.axis_index("tensor")
    context = lax.axis_index("context")
    chip, core = tensor // 2, tensor % 2
    partner = chip * 2 + (1 - core)
    n_chip = n_tensor // 2
    tok = query.shape[0]
    half = tok // 2
    cols = chunks * own.shape[-1]
    width = own.shape[-1]
    even = context % 2 == 0
    odd = context % 2 == 1
    ahead = context + 2 < n_context
    first_kv = tensor * (kv_count * per_kv) // (H // KVH) if per_kv * kv_count < H // KVH else tensor * kv_count

    def place(d):
        return (REACH - d) * tok

    kv_loads = []
    for g in range(kv_count):
        at = pl.ds(pl.multiple_of((first_kv + g) * HD, HD), HD)
        mine = kv.at[g, pl.ds(place(0), tok)]
        pair = (
            pltpu.make_async_copy(key_hbm.at[:, at], mine.at[:, pl.ds(0, HD)], kv_load_sem.at[g, 0]),
            pltpu.make_async_copy(value_hbm.at[:, at], mine.at[:, pl.ds(HD, HD)], kv_load_sem.at[g, 1]),
        )
        for c in pair:
            c.start()
        kv_loads.append(pair)
    query_load = pltpu.make_async_copy(query_hbm, query, load_sem)
    query_load.start()

    barrier = pltpu.get_barrier_semaphore()
    heard = jnp.int32(n_chip)
    for d in range(1, REACH + 1):
        for away in (d, -d):
            there = context + away
            ok = (there >= 0) & (there < n_context)
            heard = heard + jnp.where(ok, 1, 0).astype(jnp.int32)

            @pl.when(ok)
            def _():
                pl.semaphore_signal(barrier, inc=1, device_id={"tensor": tensor, "context": there}, device_id_type=MESH)

    pl.semaphore_signal(barrier, inc=1, device_id={"tensor": partner, "context": context}, device_id_type=MESH)
    for d in range(1, n_chip):
        to = lax.rem(chip + d, n_chip) * 2 + core
        pl.semaphore_signal(barrier, inc=1, device_id={"tensor": to, "context": context}, device_id_type=MESH)
    pl.semaphore_wait(barrier, heard)

    parts = 2 * kv_count
    by_even = range(parts // 2)
    by_odd = range(parts // 2, parts)
    later_first = sorted(range(parts), key=lambda q: 1 - q % 2)

    def kv_copy(q, from_d, to_d, kind, there):
        g, h = q // 2, q % 2
        return pltpu.make_async_remote_copy(
            src_ref=kv.at[g, pl.ds(place(from_d) + h * half, half)],
            dst_ref=kv.at[g, pl.ds(place(to_d) + h * half, half)],
            send_sem=kv_send.at[kind, q],
            recv_sem=kv_recv.at[to_d - 1, q],
            device_id={"tensor": tensor, "context": there},
            device_id_type=MESH,
        )

    def hops(q):
        near = context >= 2
        far = context >= 4
        here = [
            (ahead, lambda: kv_copy(q, 0, 2, 0, context + 2)),
            (even, lambda: kv_copy(q, 0, 1, 1, context + 1)),
            (even & near, lambda: kv_copy(q, 2, 3, 2, context + 1)),
            (odd & near, lambda: kv_copy(q, 2, 1, 2, context - 1)),
            (near & ahead, lambda: kv_copy(q, 2, 4, 3, context + 2)),
        ]
        if q in by_even:
            here.append((even & near & ahead, lambda: kv_copy(q, 1, 3, 4, context + 2)))
        else:
            here.append((odd & far, lambda: kv_copy(q, 4, 3, 4, context - 1)))
        return here

    def launch(q, hop, *also):
        ok, c = hops(q)[hop]
        for more in also:
            ok = ok & more

        @pl.when(ok)
        def _():
            c().start()

    def arrive(d, q, *also):
        ok = context >= d
        for more in also:
            ok = ok & more

        @pl.when(ok)
        def _():
            kv_copy(q, 0, d, 0, context).wait_recv()

    def doc_copy(d):
        return pltpu.make_async_remote_copy(
            src_ref=doc_ref,
            dst_ref=docs.at[REACH - d],
            send_sem=doc_send.at[d - 1],
            recv_sem=doc_recv.at[d - 1],
            device_id={"tensor": tensor, "context": context + d},
            device_id_type=MESH,
        )

    for d in range(1, REACH + 1):
        @pl.when(context + d < n_context)
        def _():
            doc_copy(d).start()

    for g in range(kv_count):
        for c in kv_loads[g]:
            c.wait()
        for q in (2 * g, 2 * g + 1):
            launch(q, 0)
            launch(q, 1)

    def weight_copy(i, side):
        to = lax.rem(chip + 1 + i // chunks, n_chip) * 2 + (core if side == 0 else 1 - core)
        at = to * cols + lax.rem(i, chunks) * width
        return pltpu.make_async_copy(
            weight_hbm.at[:, pl.ds(pl.multiple_of(at, 128), width)], weight.at[i, side], weight_sem.at[i, side]
        )

    @pl.loop(0, steps)
    def _(i):
        weight_copy(i, 1).start()
        weight_copy(i, 0).start()

    scale = HD ** -0.5 * math.log2(math.e)

    def columns(head):
        return pl.ds(pl.multiple_of(head * HD, HD), HD)

    def attend(g, h, r, start, size, first, last):
        rows = pl.ds(r * half, half)
        keys = pl.ds(start, size)
        heads = (g * per_kv + 2 * h, g * per_kv + 2 * h + 1)
        at = g * (per_kv // 2) + h
        q = jnp.concatenate([query[rows, columns(head)] for head in heads], axis=0)
        scores = lax.dot_general(
            q, kv[g, keys, :HD], (((1,), (1,)), ((), ())), preferred_element_type=jnp.float32
        ) + jnp.concatenate([bias[rows, keys]] * 2, axis=0)
        top = jnp.max(scores, axis=-1, keepdims=True)
        if not first:
            before = run_top[at, r][:, :1]
            top = jnp.maximum(top, before)
        values = kv[g, keys, HD:]
        both = jnp.concatenate([values, jnp.ones_like(values)], axis=1)
        p = jnp.exp2((scores - top) * scale).astype(jnp.bfloat16)
        sums = jnp.dot(p, both, preferred_element_type=jnp.float32)
        if not first:
            sums = sums + jnp.exp2((before - top) * scale) * run_sum[at, r]
        if last:
            done = (sums[:, :HD] / sums[:, HD:]).astype(jnp.bfloat16)
            att[rows, columns(heads[0])] = done[:half]
            att[rows, columns(heads[1])] = done[half:]
        else:
            run_top[at, r] = jnp.broadcast_to(top, (tok, HD))
            run_sum[at, r] = sums

    def attend_all(g, r, start, size, first, last):
        @pl.loop(0, per_kv // 2, unroll=min(2, per_kv // 2))
        def _(h):
            attend(g, h, r, start, size, first, last)

    doc_row = doc_ref[...].astype(jnp.float32)
    doc_col = jnp.broadcast_to(doc_row, (tok, tok)).T
    causal = lax.broadcasted_iota(jnp.int32, (tok, tok), 1) <= lax.broadcasted_iota(jnp.int32, (tok, tok), 0)
    bias[:, pl.ds(place(0), tok)] = jnp.where(causal & (doc_col == doc_row), 0.0, NEG_BIG)
    query_load.wait()
    for g in range(kv_count):
        attend_all(g, 1, place(0), tok, True, False)
        attend_all(g, 0, place(0), half, True, False)

    for d in range(1, REACH + 1):
        @pl.when(context < d)
        def _():
            docs[REACH - d] = jnp.full(docs.shape[1:], -1, jnp.int32)
            for g in range(kv_count):
                kv[g, pl.ds(place(d), tok)] = jnp.zeros((tok, 2 * HD), kv.dtype)

        @pl.when(context >= d)
        def _():
            doc_copy(d).wait_recv()

    for d in range(1, REACH + 1):
        row = docs[REACH - d].astype(jnp.float32)
        bias[:, pl.ds(place(d), tok)] = jnp.where(doc_col == row, 0.0, NEG_BIG)

    lag = 2
    for q in range(max(parts, lag + len(by_even))):
        if q < parts:
            arrive(2, q)
            launch(q, 2)
            launch(q, 3)
            if q in by_odd:
                launch(q, 4, odd)
        if q - lag in by_even:
            arrive(1, q - lag, even)
            launch(q - lag, 5)
    for q in later_first:
        launch(q, 4, even) if q in by_odd else launch(q, 4)

    def middle(g, r):
        attend_all(g, r, place(3) + tok, 2 * tok, False, False)

    def distant(g, r):
        skip = half * r
        attend_all(g, r, skip, 2 * tok - skip, False, True)

    def middle_arrive(g):
        for q in (2 * g, 2 * g + 1):
            arrive(1, q, odd) if q in by_even else arrive(1, q)

    def relay_far(q):
        arrive(4, q, odd)
        launch(q, 5)

    waiting = [(g, r) for g in range(kv_count) for r in (1, 0)]
    late = waiting.pop() if kv_count > 1 else None
    relays = list(by_odd)
    for g, r in waiting:
        if r == 1:
            middle_arrive(g)
        middle(g, r)
        if relays:
            relay_far(relays.pop(0))
    for q in relays:
        relay_far(q)

    def distant_arrive(g, r):
        if r == 1:
            arrive(3, 2 * g)
            arrive(3, 2 * g + 1)
        q = 2 * g + r
        arrive(4, q, even) if q in by_odd else arrive(4, q)

    def pair_copy(i, rows, k):
        return pltpu.make_async_remote_copy(
            src_ref=pair_out.at[i, rows], dst_ref=pair_in.at[i, rows],
            send_sem=pair_send.at[i, k], recv_sem=pair_recv.at[i, k],
            device_id={"tensor": partner, "context": context}, device_id_type=MESH,
        )

    def chip_copy(i, r):
        to = lax.rem(chip + 1 + i // chunks, n_chip) * 2 + core
        rows = pl.ds(r * half, half)
        return pltpu.make_async_remote_copy(
            src_ref=chip_out.at[i, rows], dst_ref=chip_in.at[i, rows],
            send_sem=chip_send.at[i, r], recv_sem=chip_recv.at[i, r],
            device_id={"tensor": to, "context": context}, device_id_type=MESH,
        )

    away = steps - chunks

    def project(i, rows, k, first):
        if first:
            weight_copy(i, 1).wait()
        pair_out[i, rows] = jnp.dot(att[rows, :], weight[i, 1], preferred_element_type=jnp.float32).astype(jnp.bfloat16)
        pair_copy(i, rows, k).start()
        if first:
            weight_copy(i, 0).wait()
        own[i, rows] = jnp.dot(att[rows, :], weight[i, 0], preferred_element_type=jnp.float32).astype(jnp.bfloat16)

    def forward(i, r):
        rows = pl.ds(r * half, half)
        pair_copy(i, rows, r).wait_recv()
        both = own[i, rows].astype(jnp.float32) + pair_in[i, rows].astype(jnp.float32)
        chip_out[i, rows] = both.astype(jnp.bfloat16)
        chip_copy(i, r).start()

    for r in (1, 0):
        rows = pl.ds(r * half, half)
        if r == 0 and late is not None:
            middle(*late)
        for g in range(kv_count):
            distant_arrive(g, r)
            distant(g, r)

        project(0, rows, r, r == 1)

        @pl.loop(1, away)
        def _(i):
            project(i, rows, r, r == 1)
            forward(i - 1, r)

        forward(away - 1, r)

    every = pl.ds(0, tok)
    @pl.loop(away, steps)
    def _(i):
        project(i, every, 0, True)

    for j in range(chunks):
        pair_copy(away + j, every, 0).wait_recv()
    for r in (1, 0):
        for j in range(chunks):
            rows = pl.ds(r * half, half)
            both = own[away + j, rows].astype(jnp.float32) + pair_in[away + j, rows].astype(jnp.float32)
            for d in range(n_chip - 1):
                chip_copy(d * chunks + j, r).wait_recv()
            for d in range(n_chip - 1):
                both = both + chip_in[d * chunks + j, rows].astype(jnp.float32)
            out_ref[rows, pl.ds(j * width, width)] = both.astype(out_ref.dtype)

    for d in range(1, REACH + 1):
        @pl.when(context + d < n_context)
        def _():
            doc_copy(d).wait_send()
    for q in range(parts):
        for ok, c in hops(q):
            @pl.when(ok)
            def _():
                c().wait_send()

    @pl.loop(0, away)
    def _(i):
        for r in range(2):
            pair_copy(i, pl.ds(r * half, half), r).wait_send()
            chip_copy(i, r).wait_send()

    @pl.loop(away, steps)
    def _(i):
        pair_copy(i, every, 0).wait_send()


def body(n_tensor, n_context, query_rows, key_rows, value_rows, doc_ids, out_weight):
    tok, local = query_rows.shape
    local_heads = local // HD
    group_size = H // KVH
    kv_count = max(1, local_heads // group_size)
    per_kv = local_heads // kv_count
    model = out_weight.shape[1]
    cols = model // n_tensor
    width = min(CHUNK, cols)
    chunks = cols // width
    n_chip = n_tensor // 2
    steps = n_chip * chunks
    assert n_tensor % 2 == 0 and n_context % 2 == 0 and cols % width == 0 and n_tensor > 2 and per_kv % 2 == 0 and tok % 2 == 0
    assert REACH * tok >= DOC_MOST - 1
    bf = jnp.bfloat16
    dma = pltpu.SemaphoreType.DMA
    anywhere = pl.BlockSpec(memory_space=pl.ANY)
    inside = pl.BlockSpec(memory_space=pltpu.VMEM)
    away = steps - chunks
    return pl.pallas_call(
        functools.partial(kernel, n_tensor, n_context, kv_count, per_kv, steps, chunks),
        out_shape=pltpu.VMEM((tok, cols), bf),
        in_specs=[anywhere, anywhere, anywhere, inside, anywhere],
        out_specs=inside,
        scratch_shapes=[
            pltpu.VMEM((tok, local), bf),
            pltpu.VMEM((kv_count, (REACH + 1) * tok, 2 * HD), bf),
            pltpu.VMEM((REACH, 1, tok), jnp.int32),
            pltpu.VMEM((tok, (REACH + 1) * tok), jnp.float32),
            pltpu.VMEM((local_heads // 2, 2, tok, HD), jnp.float32),
            pltpu.VMEM((local_heads // 2, 2, tok, 2 * HD), jnp.float32),
            pltpu.VMEM((tok, local), bf),
            pltpu.VMEM((steps, 2, local, width), bf),
            pltpu.VMEM((steps, tok, width), bf),
            pltpu.VMEM((steps, tok, width), bf),
            pltpu.VMEM((steps, tok, width), bf),
            pltpu.VMEM((max(away, 1), tok, width), bf),
            pltpu.VMEM((max(away, 1), tok, width), bf),
            dma,
            dma((kv_count, 2)),
            dma((steps, 2)),
            dma((5, 2 * kv_count)),
            dma((REACH, 2 * kv_count)),
            dma((REACH,)),
            dma((REACH,)),
            dma((steps, 2)),
            dma((steps, 2)),
            dma((max(away, 1), 2)),
            dma((max(away, 1), 2)),
        ],
        compiler_params=pltpu.CompilerParams(
            collective_id=0, has_side_effects=True, vmem_limit_bytes=57 * 1024 * 1024
        ),
    )(query_rows, key_rows, value_rows, doc_ids.reshape(1, tok), out_weight)


def solution(mesh):
    placed = (
        P("context", "tensor"),
        P("context", None),
        P("context", None),
        P("context"),
        P("tensor", None),
    )
    return jax.shard_map(
        functools.partial(body, mesh.shape["tensor"], mesh.shape["context"]),
        mesh=mesh, in_specs=placed, out_specs=P("context", "tensor"), check_vma=False,
    )
```

time: 55.1 us -> 50.9 us (0.924); the launches traced: 54.9 us -> 50.1 us
  Pallas kernels: 52.6 us -> 49.1 us
  local copies, waits for them, and re-layouts: 2.3 us -> 0.97 us
    pallas_call x1, Pallas kernels: 52.6 us -> 49.1 us  [body(): pl.pallas_call(functools.partial(kernel, n_tensor, n_context, kv_count, p...]
    unnamed x1, local copies, waits for them, and re-layouts: 2.3 us -> 0.97 us
where the time goes in v1:
time: 50.9 us; the launch traced here: 50.1 us
  Pallas kernels  49.1 us (96%)
  local copies, waits for them, and re-layouts  0.97 us (2%)
    pallas_call x1, Pallas kernels, body(): pl.pallas_call(functools.partial(kernel, n_tensor, n_context, kv_count, p...  49.1 us

profile of v1, /device:TPU:16, one launch (start us, length us, event | category | flops | bytes accessed | tf_op | source)
XLA Modules:
  0.0 50.1 jit_solution(10104033774317475372)
XLA Ops:
  0.0 49.1 %shard_map.55 = bf16[256,2048]{1,0:T(8,128)(2,1)S(1)} custom-call(bf16[256,2048]{1,0:T(8,128)(2,1)} %query_hbm.1, bf16[256,1024]{1,0:T(8,128)(2,1)} %key_hbm.1, bf16[256,1024]{1,0:T(8,128)(2,1)} %value_hbm.1, s32[1,256]{1,0:T(1,128)} %bitcast.1, bf16[2048,8192]{1,0:T(8,128)(2,1)} %weight_hbm.1), custom_call_target="tpu_custom_call" | custom-call | tf_op jit(solution)/shard_map/pallas_call | solution.py:378
  49.1 1.0 %copy.7 = bf16[256,2048]{1,0:T(8,128)(2,1)} copy(bf16[256,2048]{1,0:T(8,128)(2,1)S(1)} %shard_map.55) | data formatting | bytes 2097152

commit v2 on v1

--- a/solution.py
+++ b/solution.py
@@ -13,6 +13,7 @@
 HD = 128
 DOC_MOST = 1024
 REACH = 4
+CUTS = 4
 NEG_BIG = -1e30
 MESH = pl.DeviceIdType.MESH
 CHUNK = 512
@@ -57,16 +58,16 @@
     query_load.start()
 
     barrier = pltpu.get_barrier_semaphore()
-    heard = jnp.int32(n_chip)
-    for d in range(1, REACH + 1):
-        for away in (d, -d):
-            there = context + away
-            ok = (there >= 0) & (there < n_context)
-            heard = heard + jnp.where(ok, 1, 0).astype(jnp.int32)
-
-            @pl.when(ok)
-            def _():
-                pl.semaphore_signal(barrier, inc=1, device_id={"tensor": tensor, "context": there}, device_id_type=MESH)
+    beside = context + 1 - 2 * (context % 2)
+    heard = jnp.int32(n_chip + 1)
+    pl.semaphore_signal(barrier, inc=1, device_id={"tensor": tensor, "context": beside}, device_id_type=MESH)
+    for there in (context + 2, context - 2):
+        ok = (there >= 0) & (there < n_context)
+        heard = heard + jnp.where(ok, 1, 0).astype(jnp.int32)
+
+        @pl.when(ok)
+        def _():
+            pl.semaphore_signal(barrier, inc=1, device_id={"tensor": tensor, "context": there}, device_id_type=MESH)
 
     pl.semaphore_signal(barrier, inc=1, device_id={"tensor": partner, "context": context}, device_id_type=MESH)
     for d in range(1, n_chip):
@@ -74,37 +75,57 @@
         pl.semaphore_signal(barrier, inc=1, device_id={"tensor": to, "context": context}, device_id_type=MESH)
     pl.semaphore_wait(barrier, heard)
 
-    parts = 2 * kv_count
-    by_even = range(parts // 2)
-    by_odd = range(parts // 2, parts)
-    later_first = sorted(range(parts), key=lambda q: 1 - q % 2)
+    parts = CUTS * kv_count
+    piece = tok // CUTS
+    by_odd = range(parts // 4, parts - parts // 4)
+    by_even = [q for q in range(parts) if q not in by_odd]
+    later = [q for q in range(parts) if q % CUTS >= CUTS // 2]
+    near = context >= 2
+    far = context >= 4
 
     def kv_copy(q, from_d, to_d, kind, there):
-        g, h = q // 2, q % 2
+        g, t = q // CUTS, q % CUTS
         return pltpu.make_async_remote_copy(
-            src_ref=kv.at[g, pl.ds(place(from_d) + h * half, half)],
-            dst_ref=kv.at[g, pl.ds(place(to_d) + h * half, half)],
+            src_ref=kv.at[g, pl.ds(place(from_d) + t * piece, piece)],
+            dst_ref=kv.at[g, pl.ds(place(to_d) + t * piece, piece)],
             send_sem=kv_send.at[kind, q],
             recv_sem=kv_recv.at[to_d - 1, q],
             device_id={"tensor": tensor, "context": there},
             device_id_type=MESH,
         )
 
+    def doc_copy(from_d, to_d, kind, there):
+        return pltpu.make_async_remote_copy(
+            src_ref=docs.at[REACH - from_d] if from_d else doc_ref,
+            dst_ref=docs.at[REACH - to_d],
+            send_sem=doc_send.at[kind],
+            recv_sem=doc_recv.at[to_d - 1],
+            device_id={"tensor": tensor, "context": there},
+            device_id_type=MESH,
+        )
+
+    def routes(q):
+        here = [
+            (ahead, 0, 2, 0, context + 2),
+            (even, 0, 1, 1, context + 1),
+            (even & near, 2, 3, 2, context + 1),
+            (odd & near, 2, 1, 2, context - 1),
+            (near & ahead, 2, 4, 3, context + 2),
+        ]
+        if q is None or q in by_even:
+            here.append((even & near & ahead, 1, 3, 4, context + 2))
+        else:
+            here.append((odd & far, 4, 3, 4, context - 1))
+        return here
+
     def hops(q):
-        near = context >= 2
-        far = context >= 4
-        here = [
-            (ahead, lambda: kv_copy(q, 0, 2, 0, context + 2)),
-            (even, lambda: kv_copy(q, 0, 1, 1, context + 1)),
-            (even & near, lambda: kv_copy(q, 2, 3, 2, context + 1)),
-            (odd & near, lambda: kv_copy(q, 2, 1, 2, context - 1)),
-            (near & ahead, lambda: kv_copy(q, 2, 4, 3, context + 2)),
-        ]
-        if q in by_even:
-            here.append((even & near & ahead, lambda: kv_copy(q, 1, 3, 4, context + 2)))
-        else:
-            here.append((odd & far, lambda: kv_copy(q, 4, 3, 4, context - 1)))
-        return here
+        if q is None:
+            return [(ok, functools.partial(doc_copy, *way)) for ok, *way in routes(q)]
+        return [(ok, functools.partial(kv_copy, q, *way)) for ok, *way in routes(q)]
+
+    def launch_all(q, *which):
+        for hop in which:
+            launch(q, hop)
 
     def launch(q, hop, *also):
         ok, c = hops(q)[hop]
@@ -124,27 +145,21 @@
         def _():
             kv_copy(q, 0, d, 0, context).wait_recv()
 
-    def doc_copy(d):
-        return pltpu.make_async_remote_copy(
-            src_ref=doc_ref,
-            dst_ref=docs.at[REACH - d],
-            send_sem=doc_send.at[d - 1],
-            recv_sem=doc_recv.at[d - 1],
-            device_id={"tensor": tensor, "context": context + d},
-            device_id_type=MESH,
-        )
-
-    for d in range(1, REACH + 1):
-        @pl.when(context + d < n_context)
-        def _():
-            doc_copy(d).start()
-
+    def doc_arrive(d, *also):
+        ok = context >= d
+        for more in also:
+            ok = ok & more
+
+        @pl.when(ok)
+        def _():
+            doc_copy(0, d, 0, context).wait_recv()
+
+    launch_all(None, 0, 1)
     for g in range(kv_count):
         for c in kv_loads[g]:
             c.wait()
-        for q in (2 * g, 2 * g + 1):
-            launch(q, 0)
-            launch(q, 1)
+        for q in range(CUTS * g, CUTS * (g + 1)):
+            launch_all(q, 0, 1)
 
     def weight_copy(i, side):
         to = lax.rem(chip + 1 + i // chunks, n_chip) * 2 + (core if side == 0 else 1 - core)
@@ -172,26 +187,27 @@
         scores = lax.dot_general(
             q, kv[g, keys, :HD], (((1,), (1,)), ((), ())), preferred_element_type=jnp.float32
         ) + jnp.concatenate([bias[rows, keys]] * 2, axis=0)
-        top = jnp.max(scores, axis=-1, keepdims=True)
+        top = jnp.broadcast_to(jnp.max(scores, axis=-1, keepdims=True), (tok, HD))
         if not first:
-            before = run_top[at, r][:, :1]
+            before = run_top[at, r]
             top = jnp.maximum(top, before)
         values = kv[g, keys, HD:]
         both = jnp.concatenate([values, jnp.ones_like(values)], axis=1)
-        p = jnp.exp2((scores - top) * scale).astype(jnp.bfloat16)
+        p = jnp.exp2((scores - jnp.concatenate([top] * (size // HD), axis=1)) * scale).astype(jnp.bfloat16)
         sums = jnp.dot(p, both, preferred_element_type=jnp.float32)
         if not first:
-            sums = sums + jnp.exp2((before - top) * scale) * run_sum[at, r]
+            fade = jnp.exp2((before - top) * scale)
+            sums = sums + jnp.concatenate([fade, fade], axis=1) * run_sum[at, r]
         if last:
             done = (sums[:, :HD] / sums[:, HD:]).astype(jnp.bfloat16)
             att[rows, columns(heads[0])] = done[:half]
             att[rows, columns(heads[1])] = done[half:]
         else:
-            run_top[at, r] = jnp.broadcast_to(top, (tok, HD))
+            run_top[at, r] = top
             run_sum[at, r] = sums
 
     def attend_all(g, r, start, size, first, last):
-        @pl.loop(0, per_kv // 2, unroll=min(2, per_kv // 2))
+        @pl.loop(0, per_kv // 2, unroll=min(4, per_kv // 2))
         def _(h):
             attend(g, h, r, start, size, first, last)
 
@@ -202,70 +218,121 @@
     query_load.wait()
     for g in range(kv_count):
         attend_all(g, 1, place(0), tok, True, False)
-        attend_all(g, 0, place(0), half, True, False)
-
-    for d in range(1, REACH + 1):
-        @pl.when(context < d)
+        attend_all(g, 0, place(0), tok, True, False)
+
+    def mask(d, where=True):
+        @pl.when(where & (context < d))
         def _():
             docs[REACH - d] = jnp.full(docs.shape[1:], -1, jnp.int32)
             for g in range(kv_count):
                 kv[g, pl.ds(place(d), tok)] = jnp.zeros((tok, 2 * HD), kv.dtype)
 
-        @pl.when(context >= d)
-        def _():
-            doc_copy(d).wait_recv()
-
-    for d in range(1, REACH + 1):
-        row = docs[REACH - d].astype(jnp.float32)
-        bias[:, pl.ds(place(d), tok)] = jnp.where(doc_col == row, 0.0, NEG_BIG)
-
-    lag = 2
-    for q in range(max(parts, lag + len(by_even))):
-        if q < parts:
-            arrive(2, q)
-            launch(q, 2)
-            launch(q, 3)
-            if q in by_odd:
-                launch(q, 4, odd)
-        if q - lag in by_even:
-            arrive(1, q - lag, even)
-            launch(q - lag, 5)
-    for q in later_first:
-        launch(q, 4, even) if q in by_odd else launch(q, 4)
+        @pl.when(where & (context < n_context))
+        def _():
+            row = docs[REACH - d].astype(jnp.float32)
+            bias[:, pl.ds(place(d), tok)] = jnp.where(doc_col == row, 0.0, NEG_BIG)
+
+    doc_arrive(2)
+    launch_all(None, 2, 3, 4)
+    mask(2)
+
+    lag = CUTS + 1
+    sent = []
+
+    def relay_even(q):
+        arrive(1, q, even)
+        launch(q, 5)
 
     def middle(g, r):
-        attend_all(g, r, place(3) + tok, 2 * tok, False, False)
+        attend_all(g, r, place(2), 2 * tok, False, False)
 
     def distant(g, r):
         skip = half * r
         attend_all(g, r, skip, 2 * tok - skip, False, True)
 
-    def middle_arrive(g):
-        for q in (2 * g, 2 * g + 1):
-            arrive(1, q, odd) if q in by_even else arrive(1, q)
+    def middle_arrive(g, where):
+        for q in range(CUTS * g, CUTS * (g + 1)):
+            if q in by_odd:
+                arrive(1, q, where)
+                continue
+            if where is not even:
+                arrive(1, q, odd)
+            if where is not odd and q in turns:
+                turns.remove(q)
+                relay_even(q)
+
+    def odd_middle(r):
+        @pl.when(odd)
+        def _():
+            if r == 1:
+                middle_arrive(0, odd)
+            middle(0, r)
+
+    odd_turns = [(CUTS - 1, 1), (min(parts - 1, CUTS + 1), 0)]
+    turns = list(by_even)
+    queue = list(later)
+    for q in range(parts):
+        arrive(2, q)
+        launch_all(q, 2, 3)
+        if q in by_odd:
+            launch(q, 4, odd)
+        if q >= lag and turns and turns[0] <= q - lag:
+            relay_even(turns.pop(0))
+        elif queue and queue[0] <= q:
+            sent.append(queue.pop(0))
+            launch(sent[-1], 4, even)
+        if q == CUTS - 1:
+            doc_arrive(1, odd)
+            mask(1, odd)
+        for turn, r in odd_turns:
+            if q == turn:
+                odd_middle(r)
+        if q == (3 * parts) // 4:
+            doc_arrive(1, even)
+            launch(None, 5)
+    for q in sorted(by_even, key=lambda q: q not in later):
+        launch(q, 4, odd)
+    for q in queue:
+        launch(q, 4, even)
+    rest = [q for q in range(parts) if q not in later]
+    launch(rest[0], 4, even)
 
     def relay_far(q):
         arrive(4, q, odd)
         launch(q, 5)
 
-    waiting = [(g, r) for g in range(kv_count) for r in (1, 0)]
-    late = waiting.pop() if kv_count > 1 else None
     relays = list(by_odd)
-    for g, r in waiting:
-        if r == 1:
-            middle_arrive(g)
-        middle(g, r)
-        if relays:
-            relay_far(relays.pop(0))
-    for q in relays:
+    for q in relays[: len(relays) // 2]:
         relay_far(q)
+    mask(1, even)
+    doc_arrive(4)
+    mask(4)
+
+    @pl.when(even)
+    def _():
+        middle_arrive(0, even)
+        for r in (1, 0):
+            middle(0, r)
+
+    late = (kv_count - 1, 0) if kv_count > 1 else None
+    for g in range(1, kv_count):
+        middle_arrive(g, True)
+        middle(g, 1)
+        if g < kv_count - 1:
+            middle(g, 0)
+    for q in rest[1:]:
+        launch(q, 4, even)
+    for q in relays[len(relays) // 2 :]:
+        relay_far(q)
+    doc_arrive(3)
+    mask(3)
 
     def distant_arrive(g, r):
-        if r == 1:
-            arrive(3, 2 * g)
-            arrive(3, 2 * g + 1)
-        q = 2 * g + r
-        arrive(4, q, even) if q in by_odd else arrive(4, q)
+        for q in range(CUTS * g, CUTS * (g + 1)):
+            if r == 1:
+                arrive(3, q)
+            if (q in later) == (r == 1):
+                arrive(4, q, even) if q in by_odd else arrive(4, q)
 
     def pair_copy(i, rows, k):
         return pltpu.make_async_remote_copy(
@@ -285,11 +352,13 @@
 
     away = steps - chunks
 
-    def project(i, rows, k, first):
+    def give(i, rows, k, first):
         if first:
             weight_copy(i, 1).wait()
         pair_out[i, rows] = jnp.dot(att[rows, :], weight[i, 1], preferred_element_type=jnp.float32).astype(jnp.bfloat16)
         pair_copy(i, rows, k).start()
+
+    def keep(i, rows, first):
         if first:
             weight_copy(i, 0).wait()
         own[i, rows] = jnp.dot(att[rows, :], weight[i, 0], preferred_element_type=jnp.float32).astype(jnp.bfloat16)
@@ -309,22 +378,38 @@
             distant_arrive(g, r)
             distant(g, r)
 
-        project(0, rows, r, r == 1)
+        give(0, rows, r, r == 1)
+        keep(0, rows, r == 1)
 
         @pl.loop(1, away)
         def _(i):
-            project(i, rows, r, r == 1)
+            give(i, rows, r, r == 1)
             forward(i - 1, r)
+            keep(i, rows, r == 1)
 
         forward(away - 1, r)
 
     every = pl.ds(0, tok)
     @pl.loop(away, steps)
     def _(i):
-        project(i, every, 0, True)
-
-    for j in range(chunks):
-        pair_copy(away + j, every, 0).wait_recv()
+        give(i, every, 0, True)
+        keep(i, every, True)
+
+    for q in (None, *range(parts)):
+        for ok, c in hops(q):
+            @pl.when(ok)
+            def _():
+                c().wait_send()
+
+    @pl.loop(0, away)
+    def _(i):
+        for r in range(2):
+            pair_copy(i, pl.ds(r * half, half), r).wait_send()
+
+    @pl.loop(away, steps)
+    def _(i):
+        pair_copy(i, every, 0).wait()
+
     for r in (1, 0):
         for j in range(chunks):
             rows = pl.ds(r * half, half)
@@ -335,25 +420,10 @@
                 both = both + chip_in[d * chunks + j, rows].astype(jnp.float32)
             out_ref[rows, pl.ds(j * width, width)] = both.astype(out_ref.dtype)
 
-    for d in range(1, REACH + 1):
-        @pl.when(context + d < n_context)
-        def _():
-            doc_copy(d).wait_send()
-    for q in range(parts):
-        for ok, c in hops(q):
-            @pl.when(ok)
-            def _():
-                c().wait_send()
-
     @pl.loop(0, away)
     def _(i):
         for r in range(2):
-            pair_copy(i, pl.ds(r * half, half), r).wait_send()
             chip_copy(i, r).wait_send()
-
-    @pl.loop(away, steps)
-    def _(i):
-        pair_copy(i, every, 0).wait_send()
 
 
 def body(n_tensor, n_context, query_rows, key_rows, value_rows, doc_ids, out_weight):
@@ -368,7 +438,7 @@
     chunks = cols // width
     n_chip = n_tensor // 2
     steps = n_chip * chunks
-    assert n_tensor % 2 == 0 and n_context % 2 == 0 and cols % width == 0 and n_tensor > 2 and per_kv % 2 == 0 and tok % 2 == 0
+    assert n_tensor % 2 == 0 and n_context % 2 == 0 and cols % width == 0 and n_tensor > 2 and per_kv % 2 == 0 and tok % CUTS == 0
     assert REACH * tok >= DOC_MOST - 1
     bf = jnp.bfloat16
     dma = pltpu.SemaphoreType.DMA
@@ -397,9 +467,9 @@
             dma,
             dma((kv_count, 2)),
             dma((steps, 2)),
-            dma((5, 2 * kv_count)),
-            dma((REACH, 2 * kv_count)),
-            dma((REACH,)),
+            dma((5, CUTS * kv_count)),
+            dma((REACH, CUTS * kv_count)),
+            dma((5,)),
             dma((REACH,)),
             dma((steps, 2)),
             dma((steps, 2)),

time: 50.9 us -> 46.5 us (0.914); the launches traced: 50.1 us -> 46.4 us
  Pallas kernels: 49.1 us -> 45.4 us
    pallas_call x1, Pallas kernels: 49.1 us -> 45.4 us  [body(): pl.pallas_call(functools.partial(kernel, n_tensor, n_context, kv_count, p...]
where the time goes in v2:
time: 46.5 us; the launch traced here: 46.4 us
  Pallas kernels  45.4 us (98%)
  local copies, waits for them, and re-layouts  0.97 us (2%)
    pallas_call x1, Pallas kernels, body(): pl.pallas_call(functools.partial(kernel, n_tensor, n_context, kv_count, p...  45.4 us
    unnamed x1, local copies, waits for them, and re-layouts  0.97 us

profile of v2, /device:TPU:16, one launch (start us, length us, event | category | flops | bytes accessed | tf_op | source)
XLA Modules:
  0.0 46.4 jit_solution(11328115451069638195)
XLA Ops:
  0.0 45.4 %shard_map.55 = bf16[256,2048]{1,0:T(8,128)(2,1)S(1)} custom-call(bf16[256,2048]{1,0:T(8,128)(2,1)} %query_hbm.1, bf16[256,1024]{1,0:T(8,128)(2,1)} %key_hbm.1, bf16[256,1024]{1,0:T(8,128)(2,1)} %value_hbm.1, s32[1,256]{1,0:T(1,128)} %bitcast.1, bf16[2048,8192]{1,0:T(8,128)(2,1)} %weight_hbm.1), custom_call_target="tpu_custom_call" | custom-call | tf_op jit(solution)/shard_map/pallas_call | solution.py:448
  45.4 1.0 %copy.7 = bf16[256,2048]{1,0:T(8,128)(2,1)} copy(bf16[256,2048]{1,0:T(8,128)(2,1)S(1)} %shard_map.55) | data formatting | bytes 2097152
